TPU v7x, 32 devices: a whole 2x2x4 slice. The times are simulated.
32 devices in a mesh: real: 2 (over x), row: 16 (over z, y, core).
Axes of the slice: x: 2, y: 2, z: 4, core: 2. Of those that a mesh axis runs over, the one named last changes fastest.
Arguments:
- site_tensor: float32 [32, 2, 256, 256], P(('real', 'row')), parts along dimension 0, may hold values from -20 to 20
- left_env: float32 [32, 14, 256, 256], P(('real', 'row')), parts along dimension 0, may hold values from -10 to 10
- right_env: float32 [32, 14, 256, 256], P(('real', 'row')), parts along dimension 0, may hold values from -10 to 10
- sector_size: int32 [32], P('real'), parts along dimension 0, may hold values from 64 to 256
Outputs:
- left_out: float32 [32, 2, 256, 256], P(('real', 'row')), parts along dimension 0
- bond_out: float32 [32, 256, 256], P(('real', 'row')), parts along dimension 0
There are 2 independent parts, one for each index of `real`. A program takes and returns all parts, laid end to end along the dimension named above; each array names one. Nothing has to cross between parts.
All inputs are finite; a program needn't handle non-finite values.
Results may differ from a plain program's by a relative error of at most 0.00005.
Values sent between devices are 32-bit elements; how exact they have to be, the bound alone decides.
A program may use at most 64 MiB of HBM per device.

v0:
```python
import jax
import jax.numpy as jnp
from jax import lax
from jax.sharding import PartitionSpec as P

W_DN = 4
W_UP = 4


highest = lax.Precision.HIGHEST
time_step = 0.15


def padded(block, sides, width):
    for axis, dim in sides:
        count = lax.axis_size(axis)
        forward = [(i, i + 1) for i in range(count - 1)]
        backward = [(target, source) for source, target in forward]
        low = lax.ppermute(
            lax.slice_in_dim(block, block.shape[dim] - width, None, axis=dim), axis, forward
        )
        high = lax.ppermute(lax.slice_in_dim(block, 0, width, axis=dim), axis, backward)
        block = jnp.concatenate([low, block, high], axis=dim)
    return block


def shifted_2(value, axis, steps):
    count = lax.axis_size(axis)
    leading, last = (max(0, -steps), min(count, count - steps))
    return lax.ppermute(value, axis, [(source, source + steps) for source in range(leading, last)])


def apply_moved(operand, left_local, right_local, right_down, right_upper, mask_pair):
    bordered = padded(operand[None], (("row", 0),), 1)
    down_terms = jnp.einsum("ik,akl->ail", bordered[0], right_down, precision=highest)
    upper_terms = jnp.einsum("ik,akl->ail", bordered[2], right_upper, precision=highest)
    own_terms = jnp.einsum("ik,akl->ail", operand, right_local[W_DN + W_UP :], precision=highest)
    combined = jnp.concatenate([down_terms, upper_terms, own_terms], 0)
    return jnp.einsum("aij,ajl->il", left_local, combined, precision=highest) * mask_pair


def on_device(site_tensor, left_env, right_env, sector_size):
    states = site_tensor.shape[-1]
    left_local = left_env[0]
    right_local = right_env[0]
    right_down = shifted_2(right_local[:W_DN], "row", 1)
    right_upper = shifted_2(right_local[W_DN : W_DN + W_UP], "row", -1)
    own_size = lax.dynamic_index_in_dim(sector_size, lax.axis_index("row"), 0, keepdims=False)
    live_mask = (jnp.arange(states, dtype=jnp.int32) < own_size).astype(jnp.float32)
    mask_pair = live_mask[:, None] * live_mask[None, :]
    lower_source = site_tensor[0, 1] * live_mask[:, None]
    lower_block = shifted_2(lower_source, "row", 1) * live_mask[None, :]
    upper_block = site_tensor[0, 0] * mask_pair
    stacked = jnp.concatenate([upper_block, lower_block], 0)
    identity = jnp.eye(states, dtype=jnp.float32)
    gram_matrix = (
        jnp.einsum("ij,ik->jk", stacked, stacked, precision=highest)
        + identity * (1.0 - live_mask)[None, :]
    )
    factor = jnp.linalg.cholesky(gram_matrix)
    orthonormal = jax.scipy.linalg.solve_triangular(factor, stacked.T, lower=True).T
    moved_back = shifted_2(orthonormal[states:], "row", -1)
    left_out = jnp.stack([orthonormal[:states], moved_back], 0)[None]
    bond_matrix = factor.T * mask_pair

    def operator(operand):
        return apply_moved(operand, left_local, right_local, right_down, right_upper, mask_pair)

    local_norm = jnp.sum(bond_matrix * bond_matrix)
    start_norm = lax.psum(local_norm, "row")
    applied = operator(bond_matrix)
    correlation_sum = lax.psum(jnp.sum(bond_matrix * applied), "row")
    energy = correlation_sum / start_norm
    shifted = applied - energy * bond_matrix
    second = operator(shifted) - energy * shifted
    evolved = bond_matrix + time_step * shifted + 0.5 * time_step * time_step * second
    final_norm = lax.psum(jnp.sum(evolved * evolved), "row")
    return (left_out, (evolved * jnp.sqrt(start_norm / final_norm))[None])


def solution(mesh):
    placed = (
        P(("real", "row"), None, None, None),
        P(("real", "row"), None, None, None),
        P(("real", "row"), None, None, None),
        P("real"),
    )
    return jax.shard_map(
        on_device,
        mesh=mesh,
        in_specs=placed,
        out_specs=(P(("real", "row"), None, None, None), P(("real", "row"), None, None)),
        check_vma=False,
    )
```

profile of v0, /device:TPU:0, one launch (start us, length us, event | category | flops | bytes accessed | tf_op | source)
XLA Modules:
  0.0 187.4 jit_solution(6890272348640759516)
XLA Ops:
  0.6 1.2 dynamic_slice.4
  1.9 0.6 compare_convert_fusion
  2.5 1.1 fusion.86
  3.6 0.1 copy.12
  3.8 2.4 %collective-permute-start = (f32[256,256]{0,1:T(8,128)S(1)}, f32[256,256]{0,1:T(8,128)S(1)}, u32[]{:S(2)}, u32[]{:S(2)}) collective-permute-start(f32[256,256]{0,1:T(8,128)S(1)} %bitcast_multiply_fusion), channel_id=1, source_target_pairs={{0,1},{1,2},{2,3},{3,4},{4,5},{5,6},{6,7},{7,8},{8,9},{9,10},{10,1... | collective-permute-start | bytes 786440 | tf_op jit(solution)/shard_map/ppermute | solution.py:30
  6.2 3.0 %slice_bitcast_fusion.1 = (f32[4,256,256]{2,1,0:T(8,128)}, f32[4,256,256]{2,1,0:T(8,128)}) fusion(f32[1,14,256,256]{3,2,1,0:T(8,128)} %param.6), kind=kLoop, calls=%fused_computation.37 | loop fusion | bytes 4194304 | tf_op jit(solution)/shard_map/slice | solution.py:46
  9.2 1.3 collective-permute-start.5
  10.5 6.1 %collective-permute-start.3 = (f32[4,256,256]{2,1,0:T(8,128)}, f32[4,256,256]{2,1,0:T(8,128)}, u32[]{:S(2)}, u32[]{:S(2)}) collective-permute-start(f32[4,256,256]{2,1,0:T(8,128)} %get-tuple-element.26), channel_id=1, source_target_pairs={{0,1},{1,2},{2,3},{3,4},{4,5},{5,6},{6,7},{7,8},{8,9},{9,10},{10,1... | collective-permute-start | bytes 3145736 | tf_op jit(solution)/shard_map/ppermute | solution.py:30
  16.6 0.1 copy.11
  16.8 0.7 broadcast_subtract_fusion
  17.5 0.1 multiply_multiply_fusion.1
  17.6 0.6 fusion.62
  18.2 0.1 copy.8
  18.3 0.1 fusion.73
  18.4 11.7 %cholesky.49 = f32[128,128]{1,0:T(8,128)S(1)} custom-call(f32[128,128]{1,0:T(8,128)S(1)} %cholesky.115), custom_call_target="Cholesky" | custom-call | tf_op jit(solution)/shard_map/jit(cholesky)/cholesky | solution.py:60
  30.2 9.8 %custom-call.15 = f32[1,128,128]{1,2,0:T(8,128)S(1)} custom-call(f32[1,128,128]{2,1,0:T(8,128)S(1)} %get-tuple-element.35), custom_call_target="InvertDiagBlocksLowerTriangular" | custom-call | tf_op jit(solution)/shard_map/jit(cholesky)/cholesky | solution.py:60
  40.0 0.2 constant_dynamic-update-slice_fusion.1
  40.2 0.3 convolution_subtract_fusion
  40.5 11.7 %cholesky.103 = f32[128,128]{1,0:T(8,128)S(1)} custom-call(f32[128,128]{1,0:T(8,128)S(1)} %convolution_subtract_fusion), custom_call_target="Cholesky" | custom-call | tf_op jit(solution)/shard_map/jit(cholesky)/cholesky | solution.py:60
  52.3 0.6 compare_reduce_fusion
  54.1 0.8 fusion.84
  54.9 1.3 collective-permute-start.4
  56.2 4.2 %collective-permute-start.2 = (f32[1,256,256]{1,2,0:T(8,128)}, f32[1,256,256]{1,2,0:T(8,128)}, u32[]{:S(2)}, u32[]{:S(2)}) collective-permute-start(f32[1,256,256]{1,2,0:T(8,128)} %fusion.84), channel_id=1, source_target_pairs={{0,1},{1,2},{2,3},{3,4},{4,5},{5,6},{6,7},{7,8},{8,9},{9,10},{10,1... | collective-permute-start | bytes 786440 | tf_op jit(solution)/shard_map/ppermute | solution.py:19
  60.6 3.9 %while.1 = (s32[]{:T(128)}, f32[256,256]{1,0:T(8,128)S(1)}, s32[2,2]{1,0:T(2,128)S(1)}, f32[2,128,128]{2,1,0:T(8,128)S(1)}, s32[]{:T(128)}) while((s32[]{:T(128)}, f32[256,256]{1,0:T(8,128)S(1)}, s32[2,2]{1,0:T(2,128)S(1)}, f32[2,128,128]{2,1,0:T(8,128)S(1)}, s32[]{:T(128)}) %tuple.35), condition=%wide.while_cond, body=%wide.while_body.sunk | while | flops 2 | bytes 131181 | solution.py:61
  60.6 0.6 fusion.95
  61.2 1.3 bitcast_dynamic-update-slice_fusion.2
  62.6 0.6 fusion.95
  63.1 1.3 bitcast_dynamic-update-slice_fusion.2
  64.5 19.7 %custom-call.16 = f32[2,128,128]{1,2,0:T(8,128)S(1)} custom-call(f32[2,128,128]{2,1,0:T(8,128)S(1)} %get-tuple-element.9), custom_call_target="InvertDiagBlocksLowerTriangular" | custom-call | tf_op jit(solution)/shard_map/jit(_solve_triangular)/triangular_solve | solution.py:61
  84.2 0.4 fusion.64
  84.6 0.4 fusion.76
  85.0 0.4 fusion.63
  85.5 1.3 collective-permute-start.1
  86.8 4.1 %fusion.18 = f32[6,256,256]{1,2,0:T(8,128)S(1)} fusion(f32[1,14,256,256]{3,2,1,0:T(8,128)} %param.6, f32[256,256]{1,0:T(8,128)S(1)} %get-tuple-element.33, f32[256]{0:T(256)S(1)} %compare_convert_fusion, pred[]{:T(512)S(6)} %cholesky.108), kind=kOutput, calls=%fused_computation.20 | convolution fusion | flops 1208287232 | bytes 3409921 | tf_op jit(solution)/shard_map/ik,akl->ail/dot_general | solution.py:37
  91.0 1.0 copy.9
  92.0 2.9 %convolution_bitcast_fusion.2 = f32[4,256,256]{1,2,0:T(8,128)S(1)} fusion(f32[4,256,256]{2,1,0:T(8,128)S(1)} %collective-permute-done.5, f32[1,256,256]{1,2,0:T(8,128)} %collective-permute-done.4), kind=kOutput, calls=%fused_computation.26 | convolution fusion | flops 805306368 | bytes 2359296 | tf_op jit(solution)/shard_map/ik,akl->ail/dot_general | solution.py:36
  94.9 3.1 %convolution_bitcast_fusion.3 = f32[4,256,256]{1,2,0:T(8,128)S(1)} fusion(f32[4,256,256]{2,1,0:T(8,128)} %collective-permute-done.3, f32[1,256,256]{1,2,0:T(8,128)} %collective-permute-done.2), kind=kOutput, calls=%fused_computation.27 | convolution fusion | flops 805306368 | bytes 2359296 | tf_op jit(solution)/shard_map/ik,akl->ail/dot_general | solution.py:35
  98.1 3.8 %multiply_reduce_fusion.1 = (f32[]{:T(128)}, f32[]{:T(128)}, f32[256,256]{0,1:T(8,128)S(1)}) fusion(f32[256]{0:T(256)S(1)} %compare_convert_fusion, f32[256,256]{1,0:T(8,128)S(1)} %get-tuple-element.33, pred[]{:T(512)S(6)} %cholesky.108, f32[1,14,256,256]{3,2,1,0:T(8,128)S(1)} %copy-done, f32[6,256,256]{1,2,0:T(8,128)S(1)} %fusion.18, ...), kind=kOutput, calls=%fused_computation.63 | convolution fusion | flops 2821062656 | bytes 7865353 | tf_op jit(solution)/shard_map/aij,ajl->il/dot_general | solution.py:39
  101.9 34.8 %all-reduce.1 = (f32[]{:T(128)}, f32[]{:T(128)}) all-reduce(f32[]{:T(128)} %get-tuple-element.13, f32[]{:T(128)} %get-tuple-element.12), channel_id=1, replica_groups=mesh['real'=2,'row'=16] {'row'}, use_global_device_ids=true, to_apply=%region_5.6 | all-reduce | flops 2 | bytes 16 | tf_op jit(solution)/shard_map/psum | solution.py:72
  137.9 0.1 fusion.75
  138.0 1.6 collective-permute-start.6
  139.6 1.5 collective-permute-start.7
  141.1 4.1 %fusion.21 = f32[6,256,256]{1,2,0:T(8,128)S(1)} fusion(f32[1,14,256,256]{3,2,1,0:T(8,128)} %param.6, f32[256,256]{0,1:T(8,128)S(1)} %get-tuple-element.40, f32[]{:T(128)S(6)} %div.16, f32[256,256]{1,0:T(8,128)S(1)} %get-tuple-element.33, f32[256]{0:T(256)S(1)} %compare_convert_fusion, pred[]{:T(512)S(6)} %cholesky.108), kind=kOutput, calls=%fused_computation.21 | convolution fusion | flops 1208418304 | bytes 3672069 | tf_op jit(solution)/shard_map/ik,akl->ail/dot_general | solution.py:37
  145.2 3.0 %convolution_bitcast_fusion.1 = f32[4,256,256]{1,2,0:T(8,128)S(1)} fusion(f32[4,256,256]{2,1,0:T(8,128)} %collective-permute-done.3, f32[1,256,256]{1,2,0:T(8,128)S(1)} %collective-permute-done.6), kind=kOutput, calls=%fused_computation.25 | convolution fusion | flops 805306368 | bytes 2359296 | tf_op jit(solution)/shard_map/ik,akl->ail/dot_general | solution.py:35
  148.3 1.8 convolution_bitcast_fusion
  150.1 3.8 %multiply_reduce_fusion = (f32[]{:T(128)}, f32[256,256]{0,1:T(8,128)S(1)}) fusion(f32[1,14,256,256]{3,2,1,0:T(8,128)S(1)} %copy-done.1, f32[6,256,256]{1,2,0:T(8,128)S(1)} %fusion.21, f32[4,256,256]{1,2,0:T(8,128)S(1)} %convolution_bitcast_fusion, f32[4,256,256]{1,2,0:T(8,128)S(1)} %convolution_bitcast_fusion.1, f32[256,256]{0,1:T(8,128)S(1)} %get-tuple-element.40, ...), kind=kOutput, calls=%fused_computation.61 | convolution fusion | flops 2821455872 | bytes 8127497 | tf_op jit(solution)/shard_map/aij,ajl->il/dot_general | solution.py:39
  154.0 31.3 %psum.23 = f32[]{:T(128)} all-reduce(f32[]{:T(128)} %get-tuple-element.41), channel_id=1, replica_groups=mesh['real'=2,'row'=16] {'row'}, use_global_device_ids=true, to_apply=%region_9.10 | all-reduce | flops 1 | bytes 8 | tf_op jit(solution)/shard_map/psum | solution.py:77
  186.6 0.8 copy.10
  (28 shorter events, 0.5 us)
Async XLA Ops:
  3.8 13.7 %collective-permute-start = (f32[256,256]{0,1:T(8,128)S(1)}, f32[256,256]{0,1:T(8,128)S(1)}, u32[]{:S(2)}, u32[]{:S(2)}) collective-permute-start(f32[256,256]{0,1:T(8,128)S(1)} %bitcast_multiply_fusion), channel_id=1, source_target_pairs={{0,1},{1,2},{2,3},{3,4},{4,5},{5,6},{6,7},{7,8},{8,9},{9,10},{10,1... | collective-permute-start | bytes 786440 | tf_op jit(solution)/shard_map/ppermute | solution.py:30
  9.2 82.7 %collective-permute-start.5 = (f32[4,256,256]{2,1,0:T(8,128)}, f32[4,256,256]{2,1,0:T(8,128)S(1)}, u32[]{:S(2)}, u32[]{:S(2)}) collective-permute-start(f32[4,256,256]{2,1,0:T(8,128)} %get-tuple-element.27), channel_id=1, source_target_pairs={{1,0},{2,1},{3,2},{4,3},{5,4},{6,5},{7,6},{8,7},{9,8},{10,9},{11,1... | collective-permute-start | bytes 3145736 | tf_op jit(solution)/shard_map/ppermute | solution.py:30
  10.5 84.4 %collective-permute-start.3 = (f32[4,256,256]{2,1,0:T(8,128)}, f32[4,256,256]{2,1,0:T(8,128)}, u32[]{:S(2)}, u32[]{:S(2)}) collective-permute-start(f32[4,256,256]{2,1,0:T(8,128)} %get-tuple-element.26), channel_id=1, source_target_pairs={{0,1},{1,2},{2,3},{3,4},{4,5},{5,6},{6,7},{7,8},{8,9},{9,10},{10,1... | collective-permute-start | bytes 3145736 | tf_op jit(solution)/shard_map/ppermute | solution.py:30
  54.9 37.0 %collective-permute-start.4 = (f32[1,256,256]{1,2,0:T(8,128)}, f32[1,256,256]{1,2,0:T(8,128)}, u32[]{:S(2)}, u32[]{:S(2)}) collective-permute-start(f32[1,256,256]{1,2,0:T(8,128)} %fusion.84), channel_id=1, source_target_pairs={{1,0},{2,1},{3,2},{4,3},{5,4},{6,5},{7,6},{8,7},{9,8},{10,9},{11,1... | collective-permute-start | bytes 786440 | tf_op jit(solution)/shard_map/ppermute | solution.py:22
  56.2 38.7 %collective-permute-start.2 = (f32[1,256,256]{1,2,0:T(8,128)}, f32[1,256,256]{1,2,0:T(8,128)}, u32[]{:S(2)}, u32[]{:S(2)}) collective-permute-start(f32[1,256,256]{1,2,0:T(8,128)} %fusion.84), channel_id=1, source_target_pairs={{0,1},{1,2},{2,3},{3,4},{4,5},{5,6},{6,7},{7,8},{8,9},{9,10},{10,1... | collective-permute-start | bytes 786440 | tf_op jit(solution)/shard_map/ppermute | solution.py:19
  85.5 5.4 %collective-permute-start.1 = (f32[256,256]{0,1:T(8,128)S(1)}, f32[256,256]{0,1:T(8,128)S(1)}, u32[]{:S(2)}, u32[]{:S(2)}) collective-permute-start(f32[256,256]{0,1:T(8,128)S(1)} %get-tuple-element.29), channel_id=1, source_target_pairs={{1,0},{2,1},{3,2},{4,3},{5,4},{6,5},{7,6},{8,7},{9,8},{10,9},{11,1... | collective-permute-start | bytes 786440 | tf_op jit(solution)/shard_map/ppermute | solution.py:30
  92.0 6.1 %copy-start = (f32[1,14,256,256]{3,2,1,0:T(8,128)S(1)}, f32[1,14,256,256]{3,2,1,0:T(8,128)}, u32[]{:S(2)}) copy-start(f32[1,14,256,256]{3,2,1,0:T(8,128)} %param.5) | copy-start | bytes 11010052
  138.0 12.1 %copy-start.1 = (f32[1,14,256,256]{3,2,1,0:T(8,128)S(1)}, f32[1,14,256,256]{3,2,1,0:T(8,128)}, u32[]{:S(2)}) copy-start(f32[1,14,256,256]{3,2,1,0:T(8,128)} %param.5) | copy-start | bytes 11010052
  138.0 7.2 %collective-permute-start.6 = (f32[1,256,256]{1,2,0:T(8,128)S(1)}, f32[1,256,256]{1,2,0:T(8,128)S(1)}, u32[]{:S(2)}, u32[]{:S(2)}) collective-permute-start(f32[1,256,256]{1,2,0:T(8,128)S(1)} %fusion.75), channel_id=1, source_target_pairs={{0,1},{1,2},{2,3},{3,4},{4,5},{5,6},{6,7},{7,8},{8,9},{9,10},{10,1... | collective-permute-start | bytes 786440 | tf_op jit(solution)/shard_map/ppermute | solution.py:19
  139.6 8.7 %collective-permute-start.7 = (f32[1,256,256]{1,2,0:T(8,128)S(1)}, f32[1,256,256]{1,2,0:T(8,128)S(1)}, u32[]{:S(2)}, u32[]{:S(2)}) collective-permute-start(f32[1,256,256]{1,2,0:T(8,128)S(1)} %fusion.75), channel_id=1, source_target_pairs={{1,0},{2,1},{3,2},{4,3},{5,4},{6,5},{7,6},{8,7},{9,8},{10,9},{11,1... | collective-permute-start | bytes 786440 | tf_op jit(solution)/shard_map/ppermute | solution.py:22
where the time goes:
time: 188 us; the launch traced here: 187 us
  blocking collectives  66.1 us (35%)
  other arithmetic  56.2 us (30%)
  matrix products  29 us (15%)
  starting transfers between devices  19.7 us (10%)
  local copies, waits for them, and re-layouts  11.6 us (6%)
  between operations  4.75 us (3%)
    psum x1, blocking collectives, on_device(): correlation_sum = lax.psum(jnp.sum(bond_matrix * applied), 'row')  34.8 us
    another operation x6, other arithmetic, on_device(): factor = jnp.linalg.cholesky(gram_matrix)  33.9 us
    psum x1, blocking collectives, on_device(): final_norm = lax.psum(jnp.sum(evolved * evolved), 'row')  31.3 us
    another operation x3, other arithmetic, on_device(): jax.scipy.linalg.solve_triangular(factor, stacked.T, lower=True)  19.7 us
    ppermute x4, starting transfers between devices, shifted_2(): lax.ppermute(value, axis, [(source, source + steps) for source in range(l...  11.1 us
    dot_general x2, matrix products, apply_moved(): jnp.einsum('ik,akl->ail', operand, right_local[W_DN + W_UP:], precision=h...  8.2 us
    dot_general x2, matrix products, apply_moved(): jnp.einsum('aij,ajl->il', left_local, combined, precision=highest)  7.64 us
    dot_general x2, matrix products, apply_moved(): jnp.einsum('ik,akl->ail', bordered[0], right_down, precision=highest)  6.16 us
  transfers between devices with their start and end apart: 8, of which 0 were waited for; matrix products, arithmetic and copies ran while one was open for 43% of the time, Pallas kernels for 0%

commit v1 on v0

v1 whole, which is shorter than its diff:
```python
import functools

import jax
import jax.numpy as jnp
from jax import lax
from jax.experimental import pallas as pl
from jax.experimental.pallas import tpu as pltpu
from jax.sharding import PartitionSpec as P

W_DN = 4
W_UP = 4
PANEL = 16
TAU = 0.15
highest = lax.Precision.HIGHEST
f32 = jnp.float32
bf16 = jnp.bfloat16
MESH = pl.DeviceIdType.MESH


def dot(a, b):
    return jnp.dot(a, b, preferred_element_type=f32)


def split_2(value):
    high = value.astype(bf16)
    return high, (value - high.astype(f32)).astype(bf16)


def split_3(value):
    high = value.astype(bf16)
    rest = value - high.astype(f32)
    middle = rest.astype(bf16)
    return high, middle, (rest - middle.astype(f32)).astype(bf16)


def store_split(pair_ref, index, value):
    high, low = split_2(value)
    pair_ref[0, index] = high
    pair_ref[1, index] = low


def tile_sum(value):
    rows, columns = value.shape
    summed = jnp.sum(value.reshape(rows // 8, 8, columns), axis=0)
    total = summed[:, :128]
    for start in range(128, columns, 128):
        total = total + summed[:, start : start + 128]
    return total


def full_sum(tile):
    return jnp.sum(jnp.sum(tile, axis=0, keepdims=True), axis=1, keepdims=True)


def panel_step(p, lo, hi, states, aug_ref, out_ref):
    base = pl.multiple_of(p * PANEL, PANEL)
    row_id = lax.broadcasted_iota(jnp.int32, (PANEL, 128), 0)
    offset = lax.rem(p * PANEL, 128)
    diag = aug_ref[pl.ds(base, PANEL), lo : lo + 128]
    diag = pltpu.roll(diag, lax.rem(128 - offset, 128), 1)
    columns = [jnp.broadcast_to(diag[:, r : r + 1], (PANEL, 128)) for r in range(PANEL)]
    tiles = [aug_ref[pl.ds(base, PANEL), t : t + 128] for t in range(lo, hi, 128)]
    scale = jnp.zeros((PANEL, 128), f32)
    for r in range(PANEL):
        inverse = lax.rsqrt(columns[r][r : r + 1, :])
        scale = jnp.where(row_id == r, inverse, scale)
        multiplier = columns[r] * inverse
        below = jnp.where(row_id > r, multiplier, 0.0)
        for s in range(r + 1, PANEL):
            columns[s] = columns[s] - below * multiplier[s : s + 1, :]
        if r < PANEL - 1:
            tiles = [tile - below * (tile[r : r + 1, :] * inverse) for tile in tiles]
    tiles = [tile * scale for tile in tiles]
    for t, tile in zip(range(lo, hi, 128), tiles):
        out_ref[pl.ds(base, PANEL), t : t + 128] = tile
    panel = jnp.concatenate(tiles, 1)
    q1, q2, q3 = split_3(panel)
    p1, p2, p3 = (q[:, : states - lo] for q in (q1, q2, q3))
    left = jnp.concatenate([p1, p1, p2, p2, p1, p3], 0)
    right = jnp.concatenate([q1, q2, q1, q2, q3, q1], 0)
    update = lax.dot_general(left, right, (((0,), (0,)), ((), ())), preferred_element_type=f32)
    aug_ref[lo:states, lo:hi] -= update


def kernel(
    size_ref, site_hbm, left_hbm, right_hbm,
    out_hbm, bond_out,
    site, low, left_f, right_f, left_s, right_s, aug, fac, bond, applied, acc, field_in, low_out, up_out,
    red_in, red_own, local_sem, send_sem, recv_sem, red_send, red_recv,
):
    count = lax.axis_size("row")
    me = lax.axis_index("row")
    states = site.shape[-1]
    channels = left_f.shape[0]
    moved = W_DN + W_UP
    not_first, not_last = me > 0, me < count - 1

    loads = [
        pltpu.make_async_copy(site_hbm.at[0], site, local_sem.at[0]),
        pltpu.make_async_copy(left_hbm.at[0], left_f, local_sem.at[1]),
        pltpu.make_async_copy(right_hbm.at[0, moved:], right_f.at[moved:], local_sem.at[2]),
    ]
    for load in loads:
        load.start()

    barrier = pltpu.get_barrier_semaphore()
    for step in range(1, count):
        peer = lax.rem(me + step, count)
        pl.semaphore_signal(barrier, inc=1, device_id={"row": peer}, device_id_type=MESH)
    pl.semaphore_wait(barrier, count - 1)

    def remote(source, target, slot, peer):
        return pltpu.make_async_remote_copy(
            src_ref=source, dst_ref=target, send_sem=send_sem.at[slot], recv_sem=recv_sem.at[slot],
            device_id={"row": peer}, device_id_type=MESH,
        )

    to_right, to_left = jnp.minimum(me + 1, count - 1), jnp.maximum(me - 1, 0)
    send_site = remote(site_hbm.at[0, 1], low, 0, to_right)
    send_down = remote(right_hbm.at[0, :W_DN], right_f.at[:W_DN], 1, to_right)
    send_up = remote(right_hbm.at[0, W_DN:moved], right_f.at[W_DN:moved], 2, to_left)
    send_low = remote(low_out, out_hbm.at[0, 1], 3, to_left)
    fields = [bond, applied]
    send_fields = [
        (remote(fields[t], field_in.at[t, 0], 4 + 2 * t, to_right), remote(fields[t], field_in.at[t, 1], 5 + 2 * t, to_left))
        for t in range(2)
    ]

    @pl.when(not_last)
    def _():
        send_site.start()
        send_down.start()

    @pl.when(not_first)
    def _():
        send_up.start()

    @pl.when(me == 0)
    def _():
        low[...] = jnp.zeros_like(low)
        right_f[:W_DN] = jnp.zeros((W_DN, states, states), f32)
        field_in[:, 0] = jnp.zeros((2, states, states), f32)

    @pl.when(me == count - 1)
    def _():
        right_f[W_DN:moved] = jnp.zeros((W_UP, states, states), f32)
        field_in[:, 1] = jnp.zeros((2, states, states), f32)

    size = size_ref[me]
    size_before = size_ref[to_left]
    row = lax.broadcasted_iota(jnp.int32, (states, states), 0)
    column = lax.broadcasted_iota(jnp.int32, (states, states), 1)
    live_pair = (row < size) & (column < size)
    gram_dims = (((0,), (0,)), ((), ()))
    loads[0].wait()
    upper = jnp.where(live_pair, site[0], 0.0)
    site[0] = upper
    gram = lax.dot_general(upper, upper, gram_dims, precision=highest, preferred_element_type=f32)
    gram = gram + jnp.where((row == column) & (row >= size), 1.0, 0.0)
    aug[:, states:] = jnp.where(row == column, 1.0, 0.0).astype(f32)

    @pl.when(not_first)
    def _():
        send_site.wait_recv()

    lower = jnp.where((row < size_before) & (column < size), low[...], 0.0)
    site[1] = lower
    aug[:, :states] = gram + lax.dot_general(lower, lower, gram_dims, precision=highest, preferred_element_type=f32)
    fac[...] = jnp.zeros_like(fac)
    loads[1].wait()
    loads[2].wait()

    half = states // 2
    halves = half // PANEL

    def first_half(p, carry):
        panel_step(p, 0, states + half, states, aug, fac)
        store_split(left_s, p, left_f[p])
        return carry

    def second_half(p, carry):
        panel_step(p, half, 2 * states, states, aug, fac)
        other = jnp.minimum(p, channels - 1)
        store_split(left_s, other, left_f[other])
        mine = jnp.minimum(p - halves + moved, channels - 1)
        store_split(right_s, mine, right_f[mine])
        return carry

    lax.fori_loop(0, halves, first_half, 0)
    lax.fori_loop(halves, 2 * halves, second_half, 0)

    bond[...] = jnp.where(live_pair & (column >= row), fac[:, :states], 0.0)

    @pl.when(not_last)
    def _():
        send_fields[0][0].start()

    @pl.when(not_first)
    def _():
        send_fields[0][1].start()

    inverse = jnp.where(column <= row, fac[:, states:], 0.0)
    turned = (((1,), (1,)), ((), ()))
    low_out[...] = lax.dot_general(site[1], inverse, turned, precision=highest, preferred_element_type=f32)

    @pl.when(not_first)
    def _():
        send_low.start()

    up_out[...] = lax.dot_general(site[0], inverse, turned, precision=highest, preferred_element_type=f32)
    store_up = pltpu.make_async_copy(up_out, out_hbm.at[0, 0], local_sem.at[3])
    store_up.start()

    @pl.when(not_first)
    def _():
        send_down.wait_recv()

    @pl.when(not_last)
    def _():
        send_up.wait_recv()

    def split_moved(a, carry):
        store_split(right_s, a, right_f[a])
        return carry

    lax.fori_loop(0, moved, split_moved, 0)

    def add_channels(field, start, stop):
        high, low_part = split_2(field)
        group = 2 if (stop - start) % 2 == 0 else 1

        def some(g, carry):
            total = acc[...]
            for k in range(group):
                a = start + g * group + k
                r_high, r_low = right_s[0, a], right_s[1, a]
                l_high, l_low = left_s[0, a], left_s[1, a]
                middle = dot(high, r_high) + dot(high, r_low) + dot(low_part, r_high)
                m_high, m_low = split_2(middle)
                total = total + dot(l_high, m_high) + dot(l_high, m_low) + dot(l_low, m_high)
            acc[...] = total
            return carry

        lax.fori_loop(0, (stop - start) // group, some, 0)

    def operator(t):
        acc[...] = jnp.zeros_like(acc)
        add_channels(fields[t][...], moved, channels)

        @pl.when(not_first)
        def _():
            send_fields[t][0].wait_recv()

        add_channels(field_in[t, 0], 0, W_DN)

        @pl.when(not_last)
        def _():
            send_fields[t][1].wait_recv()

        add_channels(field_in[t, 1], W_DN, moved)

    def reductions(t):
        for step in range(1, count):
            peer = lax.rem(me + step, count)
            yield pltpu.make_async_remote_copy(
                src_ref=red_own.at[t], dst_ref=red_in.at[t, step],
                send_sem=red_send.at[t, step], recv_sem=red_recv.at[t, step],
                device_id={"row": peer}, device_id_type=MESH,
            )

    operator(0)
    applied[...] = jnp.where(live_pair, acc[...], 0.0)

    @pl.when(not_last)
    def _():
        send_fields[1][0].start()

    @pl.when(not_first)
    def _():
        send_fields[1][1].start()

    red_own[0, :8] = tile_sum(bond[...] * bond[...])
    red_own[0, 8:] = tile_sum(bond[...] * applied[...])
    first_sums = list(reductions(0))
    for one in first_sums:
        one.start()

    operator(1)

    def collect(t, copies):
        total = red_own[t]
        for step, one in enumerate(copies, 1):
            one.wait_recv()
            total = total + red_in[t, step]
        return total

    total = collect(0, first_sums)
    start_norm = full_sum(total[:8])
    energy = full_sum(total[8:]) / start_norm
    shifted = applied[...] - energy * bond[...]
    second = jnp.where(live_pair, acc[...], 0.0) - energy * applied[...] - energy * shifted
    acc[...] = bond[...] + TAU * shifted + (0.5 * TAU * TAU) * second
    red_own[1, :8] = tile_sum(acc[...] * acc[...])
    red_own[1, 8:] = jnp.zeros((8, 128), f32)
    second_sums = list(reductions(1))
    for one in second_sums:
        one.start()

    @pl.when(not_last)
    def _():
        for one in (send_site, send_down, send_fields[0][0], send_fields[1][0]):
            one.wait_send()
        send_low.wait_recv()

    @pl.when(not_first)
    def _():
        for one in (send_up, send_low, send_fields[0][1], send_fields[1][1]):
            one.wait_send()

    @pl.when(me == count - 1)
    def _():
        low[...] = jnp.zeros_like(low)
        clear = pltpu.make_async_copy(low, out_hbm.at[0, 1], local_sem.at[4])
        clear.start()
        clear.wait()

    store_up.wait()
    final_norm = full_sum(collect(1, second_sums)[:8])
    bond_out[0] = acc[...] * jnp.sqrt(start_norm / final_norm)
    for one in first_sums + second_sums:
        one.wait_send()


def on_device(site_tensor, left_env, right_env, sector_size):
    states = site_tensor.shape[-1]
    channels = left_env.shape[1]
    count = lax.axis_size("row")
    block = (states, states)
    anywhere = pl.BlockSpec(memory_space=pl.ANY)
    return pl.pallas_call(
        kernel,
        out_shape=(
            jax.ShapeDtypeStruct(site_tensor.shape, f32),
            jax.ShapeDtypeStruct((1,) + block, f32),
        ),
        in_specs=[pl.BlockSpec(memory_space=pltpu.SMEM), anywhere, anywhere, anywhere],
        out_specs=(anywhere, pl.BlockSpec(memory_space=pltpu.VMEM)),
        scratch_shapes=[
            pltpu.VMEM((2,) + block, f32),
            pltpu.VMEM(block, f32),
            pltpu.VMEM((channels,) + block, f32),
            pltpu.VMEM((channels,) + block, f32),
            pltpu.VMEM((2, channels) + block, bf16),
            pltpu.VMEM((2, channels) + block, bf16),
            pltpu.VMEM((states, 2 * states), f32),
            pltpu.VMEM((states, 2 * states), f32),
            pltpu.VMEM(block, f32),
            pltpu.VMEM(block, f32),
            pltpu.VMEM(block, f32),
            pltpu.VMEM((2, 2) + block, f32),
            pltpu.VMEM(block, f32),
            pltpu.VMEM(block, f32),
            pltpu.VMEM((2, count, 16, 128), f32),
            pltpu.VMEM((2, 16, 128), f32),
            pltpu.SemaphoreType.DMA((5,)),
            pltpu.SemaphoreType.DMA((8,)),
            pltpu.SemaphoreType.DMA((8,)),
            pltpu.SemaphoreType.DMA((2, count)),
            pltpu.SemaphoreType.DMA((2, count)),
        ],
        compiler_params=pltpu.CompilerParams(
            collective_id=0, has_side_effects=True, vmem_limit_bytes=56 * 1024 * 1024
        ),
        name="bond_update",
    )(sector_size, site_tensor, left_env, right_env)


def solution(mesh):
    placed = (
        P(("real", "row"), None, None, None),
        P(("real", "row"), None, None, None),
        P(("real", "row"), None, None, None),
        P("real"),
    )
    return jax.shard_map(
        on_device,
        mesh=mesh,
        in_specs=placed,
        out_specs=(P(("real", "row"), None, None, None), P(("real", "row"), None, None)),
        check_vma=False,
    )
```

time: 188 us -> 65.8 us (0.35)
  blocking collectives: 66.1 us -> 0 us
  Pallas kernels: 0 us -> 61.4 us
  other arithmetic: 56.2 us -> 0 us
  matrix products: 29 us -> 0 us
  starting transfers between devices: 19.7 us -> 0 us
  local copies, waits for them, and re-layouts: 11.6 us -> 3.54 us
  between operations: 4.75 us -> 0.64 us
    psum x2 -> x0, blocking collectives: 66.1 us -> none  [the longest x1 34.8 us: on_device(): correlation_sum = lax.psum(jnp.sum(bond_matrix * applied), 'row')]
    pallas_call x0 -> x1, Pallas kernels: none -> 61.4 us  [on_device(): pl.pallas_call(kernel, out_shape=(jax.ShapeDtypeStruct(site_tensor.shape,...]
    another operation x9 -> x0, other arithmetic: 53.7 us -> none  [the longest x6 33.9 us: on_device(): factor = jnp.linalg.cholesky(gram_matrix)]
    dot_general x9 -> x0, matrix products: 27.3 us -> none  [the longest x2 8.2 us: apply_moved(): jnp.einsum('ik,akl->ail', operand, right_local[W_DN + W_UP:], precision=h...]
    ppermute x8 -> x0, starting transfers between devices: 19.7 us -> none  [the longest x4 11.1 us: shifted_2(): lax.ppermute(value, axis, [(source, source + steps) for source in range(l...]
    slice x2 -> x0, local copies, waits for them, and re-layouts: 4.1 us -> none  [the longest x1 3.03 us: on_device(): right_down = shifted_2(right_local[:W_DN], 'row', 1)]
    another operation x10 -> x0, local copies, waits for them, and re-layouts: 4.02 us -> none
  transfers between devices with their start and end apart: 8 -> 0, of which waited for: 0 -> 0; matrix products, arithmetic and copies ran while one was open for 43% -> 0% of each run, Pallas kernels for 0% -> 0%
where the time goes in v1:
time: 65.8 us; the launch traced here: 65.6 us
  Pallas kernels  61.4 us (93%)
  local copies, waits for them, and re-layouts  3.54 us (5%)
    pallas_call x1, Pallas kernels, on_device(): pl.pallas_call(kernel, out_shape=(jax.ShapeDtypeStruct(site_tensor.shape,...  61.4 us
    unnamed x2, local copies, waits for them, and re-layouts  3.54 us

profile of v1, /device:TPU:0, one launch (start us, length us, event | category | flops | bytes accessed | tf_op | source)
XLA Modules:
  0.0 65.6 jit_solution(6121560720536551160)
XLA Ops:
  0.6 61.4 %bond_update.1 = (f32[1,2,256,256]{3,2,1,0:T(8,128)}, f32[1,256,256]{2,1,0:T(8,128)}) custom-call(s32[16]{0:T(128)} %size_ref.1, f32[1,2,256,256]{3,2,1,0:T(8,128)} %site_hbm.1, f32[1,14,256,256]{3,2,1,0:T(8,128)} %left_hbm.1, f32[1,14,256,256]{3,2,1,0:T(8,128)} %right_hbm.1), custom_call_target="tpu_custom_call" | custom-call | tf_op jit(solution)/shard_map/bond_update/pallas_call | solution.py:340
  62.1 1.9 %copy.8 = f32[1,2,256,256]{3,2,1,0:T(8,128)} copy(f32[1,2,256,256]{3,2,1,0:T(8,128)} %get-tuple-element.4) | data formatting | bytes 1048576
  64.0 1.7 %copy.9 = f32[1,256,256]{2,1,0:T(8,128)} copy(f32[1,256,256]{2,1,0:T(8,128)} %get-tuple-element.5) | data formatting | bytes 524288

commit v2 on v1

--- a/solution.py
+++ b/solution.py
@@ -85,7 +85,7 @@
 def kernel(
     size_ref, site_hbm, left_hbm, right_hbm,
     out_hbm, bond_out,
-    site, low, left_f, right_f, left_s, right_s, aug, fac, bond, applied, acc, field_in, low_out, up_out,
+    site, low, left_f, right_f, left_s, right_s, aug, fac, packed, bond, applied, acc, field_in, field_s, low_out, up_out,
     red_in, red_own, local_sem, send_sem, recv_sem, red_send, red_recv,
 ):
     count = lax.axis_size("row")
@@ -116,24 +116,24 @@
         )
 
     to_right, to_left = jnp.minimum(me + 1, count - 1), jnp.maximum(me - 1, 0)
+    half = states // 2
     send_site = remote(site_hbm.at[0, 1], low, 0, to_right)
-    send_down = remote(right_hbm.at[0, :W_DN], right_f.at[:W_DN], 1, to_right)
-    send_up = remote(right_hbm.at[0, W_DN:moved], right_f.at[W_DN:moved], 2, to_left)
-    send_low = remote(low_out, out_hbm.at[0, 1], 3, to_left)
-    fields = [bond, applied]
-    send_fields = [
-        (remote(fields[t], field_in.at[t, 0], 4 + 2 * t, to_right), remote(fields[t], field_in.at[t, 1], 5 + 2 * t, to_left))
-        for t in range(2)
+    send_down = [remote(right_hbm.at[0, a], right_f.at[a], 1 + a, to_right) for a in range(W_DN)]
+    send_up = [remote(right_hbm.at[0, a], right_f.at[a], 1 + a, to_left) for a in range(W_DN, moved)]
+    send_bond_right = [
+        remote(packed.at[:half], field_in.at[0, 0, :half], moved + 1, to_right),
+        remote(packed.at[half:, half:], field_in.at[0, 0, half:, half:], moved + 2, to_right),
     ]
+    send_bond_left = remote(packed, field_in.at[0, 1], moved + 3, to_left)
+    send_applied_right = remote(applied, field_in.at[1, 0], moved + 4, to_right)
+    send_applied_left = remote(applied, field_in.at[1, 1], moved + 5, to_left)
+    rightward = [send_site] + send_down + send_bond_right + [send_applied_right]
+    leftward = send_up + [send_bond_left, send_applied_left]
+    early_down, early_up = W_DN // 2, W_UP // 2
 
     @pl.when(not_last)
     def _():
         send_site.start()
-        send_down.start()
-
-    @pl.when(not_first)
-    def _():
-        send_up.start()
 
     @pl.when(me == 0)
     def _():
@@ -148,6 +148,7 @@
 
     size = size_ref[me]
     size_before = size_ref[to_left]
+    size_after = size_ref[to_right]
     row = lax.broadcasted_iota(jnp.int32, (states, states), 0)
     column = lax.broadcasted_iota(jnp.int32, (states, states), 1)
     live_pair = (row < size) & (column < size)
@@ -159,18 +160,24 @@
     gram = gram + jnp.where((row == column) & (row >= size), 1.0, 0.0)
     aug[:, states:] = jnp.where(row == column, 1.0, 0.0).astype(f32)
 
-    @pl.when(not_first)
-    def _():
+    @pl.when(not_last)
+    def _():
+        send_site.wait_send()
+        for one in send_down[:early_down]:
+            one.start()
+
+    @pl.when(not_first)
+    def _():
+        for one in send_up[:early_up]:
+            one.start()
         send_site.wait_recv()
 
     lower = jnp.where((row < size_before) & (column < size), low[...], 0.0)
-    site[1] = lower
     aug[:, :states] = gram + lax.dot_general(lower, lower, gram_dims, precision=highest, preferred_element_type=f32)
     fac[...] = jnp.zeros_like(fac)
     loads[1].wait()
     loads[2].wait()
 
-    half = states // 2
     halves = half // PANEL
 
     def first_half(p, carry):
@@ -189,75 +196,97 @@
     lax.fori_loop(0, halves, first_half, 0)
     lax.fori_loop(halves, 2 * halves, second_half, 0)
 
+    packed[...] = jnp.where(column >= row, fac[:, :states], fac[:, states:])
+
+    @pl.when(not_last)
+    def _():
+        for one in send_bond_right + send_down[early_down:]:
+            one.start()
+
+    @pl.when(not_first)
+    def _():
+        for one in [send_bond_left] + send_up[early_up:]:
+            one.start()
+
     bond[...] = jnp.where(live_pair & (column >= row), fac[:, :states], 0.0)
-
-    @pl.when(not_last)
-    def _():
-        send_fields[0][0].start()
-
-    @pl.when(not_first)
-    def _():
-        send_fields[0][1].start()
-
     inverse = jnp.where(column <= row, fac[:, states:], 0.0)
     turned = (((1,), (1,)), ((), ()))
-    low_out[...] = lax.dot_general(site[1], inverse, turned, precision=highest, preferred_element_type=f32)
-
-    @pl.when(not_first)
-    def _():
-        send_low.start()
-
     up_out[...] = lax.dot_general(site[0], inverse, turned, precision=highest, preferred_element_type=f32)
     store_up = pltpu.make_async_copy(up_out, out_hbm.at[0, 0], local_sem.at[3])
     store_up.start()
 
-    @pl.when(not_first)
-    def _():
-        send_down.wait_recv()
-
-    @pl.when(not_last)
-    def _():
-        send_up.wait_recv()
-
-    def split_moved(a, carry):
-        store_split(right_s, a, right_f[a])
-        return carry
-
-    lax.fori_loop(0, moved, split_moved, 0)
-
-    def add_channels(field, start, stop):
-        high, low_part = split_2(field)
+    def put_field(which, value):
+        field_s[which, 0], field_s[which, 1] = split_2(value)
+
+    def add_terms(total, which, a):
+        high, low_part = field_s[which, 0], field_s[which, 1]
+        r_high, r_low = right_s[0, a], right_s[1, a]
+        l_high, l_low = left_s[0, a], left_s[1, a]
+        middle = dot(high, r_high) + dot(high, r_low) + dot(low_part, r_high)
+        m_high, m_low = split_2(middle)
+        return total + dot(l_high, m_high) + dot(l_high, m_low) + dot(l_low, m_high)
+
+    def add_range(which, start, stop):
         group = 2 if (stop - start) % 2 == 0 else 1
 
         def some(g, carry):
             total = acc[...]
             for k in range(group):
-                a = start + g * group + k
-                r_high, r_low = right_s[0, a], right_s[1, a]
-                l_high, l_low = left_s[0, a], left_s[1, a]
-                middle = dot(high, r_high) + dot(high, r_low) + dot(low_part, r_high)
-                m_high, m_low = split_2(middle)
-                total = total + dot(l_high, m_high) + dot(l_high, m_low) + dot(l_low, m_high)
+                total = add_terms(total, which, start + g * group + k)
             acc[...] = total
             return carry
 
         lax.fori_loop(0, (stop - start) // group, some, 0)
 
-    def operator(t):
-        acc[...] = jnp.zeros_like(acc)
-        add_channels(fields[t][...], moved, channels)
-
+    def take_moved(down, up):
         @pl.when(not_first)
         def _():
-            send_fields[t][0].wait_recv()
-
-        add_channels(field_in[t, 0], 0, W_DN)
+            for a in down:
+                send_down[a].wait_recv()
 
         @pl.when(not_last)
         def _():
-            send_fields[t][1].wait_recv()
-
-        add_channels(field_in[t, 1], W_DN, moved)
+            for a in up:
+                send_up[a - W_DN].wait_recv()
+
+        for a in (*down, *up):
+            store_split(right_s, a, right_f[a])
+
+    acc[...] = jnp.zeros_like(acc)
+    put_field(0, bond[...])
+    add_range(0, moved, channels)
+    take_moved(range(early_down), range(W_DN, W_DN + early_up))
+
+    @pl.when(not_first)
+    def _():
+        for one in send_bond_right:
+            one.wait_recv()
+
+    put_field(1, jnp.where((column >= row) & (row < size_before) & (column < size_before), field_in[0, 0], 0.0))
+    add_range(1, 0, early_down)
+
+    @pl.when(not_last)
+    def _():
+        send_bond_left.wait_recv()
+
+    near = field_in[0, 1]
+    put_field(2, jnp.where((column >= row) & (row < size_after) & (column < size_after), near, 0.0))
+    add_range(2, W_DN, W_DN + early_up)
+    near_inverse = jnp.where(column < row, near, jnp.where(column == row, 1.0 / near, 0.0))
+    outer = jnp.where((row < size) & (column < size_after), site[1], 0.0)
+    outer = lax.dot_general(outer, near_inverse, turned, precision=highest, preferred_element_type=f32)
+    low_out[...] = jnp.where(not_last, outer, 0.0)
+    store_low = pltpu.make_async_copy(low_out, out_hbm.at[0, 1], local_sem.at[4])
+    store_low.start()
+    for k in range(max(W_DN - early_down, W_UP - early_up)):
+        down = [early_down + k] if early_down + k < W_DN else []
+        up = [W_DN + early_up + k] if early_up + k < W_UP else []
+        take_moved(down, up)
+        total = acc[...]
+        for which, group in ((1, down), (2, up)):
+            for a in group:
+                total = add_terms(total, which, a)
+        acc[...] = total
 
     def reductions(t):
         for step in range(1, count):
@@ -268,16 +297,15 @@
                 device_id={"row": peer}, device_id_type=MESH,
             )
 
-    operator(0)
     applied[...] = jnp.where(live_pair, acc[...], 0.0)
 
     @pl.when(not_last)
     def _():
-        send_fields[1][0].start()
-
-    @pl.when(not_first)
-    def _():
-        send_fields[1][1].start()
+        send_applied_right.start()
+
+    @pl.when(not_first)
+    def _():
+        send_applied_left.start()
 
     red_own[0, :8] = tile_sum(bond[...] * bond[...])
     red_own[0, 8:] = tile_sum(bond[...] * applied[...])
@@ -285,7 +313,23 @@
     for one in first_sums:
         one.start()
 
-    operator(1)
+    acc[...] = jnp.zeros_like(acc)
+    put_field(0, applied[...])
+    add_range(0, moved, channels)
+
+    @pl.when(not_first)
+    def _():
+        send_applied_right.wait_recv()
+
+    put_field(1, field_in[1, 0])
+    add_range(1, 0, W_DN)
+
+    @pl.when(not_last)
+    def _():
+        send_applied_left.wait_recv()
+
+    put_field(2, field_in[1, 1])
+    add_range(2, W_DN, moved)
 
     def collect(t, copies):
         total = red_own[t]
@@ -308,22 +352,15 @@
 
     @pl.when(not_last)
     def _():
-        for one in (send_site, send_down, send_fields[0][0], send_fields[1][0]):
+        for one in rightward[1:]:
             one.wait_send()
-        send_low.wait_recv()
-
-    @pl.when(not_first)
-    def _():
-        for one in (send_up, send_low, send_fields[0][1], send_fields[1][1]):
+
+    @pl.when(not_first)
+    def _():
+        for one in leftward:
             one.wait_send()
 
-    @pl.when(me == count - 1)
-    def _():
-        low[...] = jnp.zeros_like(low)
-        clear = pltpu.make_async_copy(low, out_hbm.at[0, 1], local_sem.at[4])
-        clear.start()
-        clear.wait()
-
+    store_low.wait()
     store_up.wait()
     final_norm = full_sum(collect(1, second_sums)[:8])
     bond_out[0] = acc[...] * jnp.sqrt(start_norm / final_norm)
@@ -357,14 +394,16 @@
             pltpu.VMEM(block, f32),
             pltpu.VMEM(block, f32),
             pltpu.VMEM(block, f32),
+            pltpu.VMEM(block, f32),
             pltpu.VMEM((2, 2) + block, f32),
+            pltpu.VMEM((3, 2) + block, bf16),
             pltpu.VMEM(block, f32),
             pltpu.VMEM(block, f32),
             pltpu.VMEM((2, count, 16, 128), f32),
             pltpu.VMEM((2, 16, 128), f32),
             pltpu.SemaphoreType.DMA((5,)),
-            pltpu.SemaphoreType.DMA((8,)),
-            pltpu.SemaphoreType.DMA((8,)),
+            pltpu.SemaphoreType.DMA((W_DN + W_UP + 6,)),
+            pltpu.SemaphoreType.DMA((W_DN + W_UP + 6,)),
             pltpu.SemaphoreType.DMA((2, count)),
             pltpu.SemaphoreType.DMA((2, count)),
         ],

time: 65.8 us -> 62.3 us (0.947)
  Pallas kernels: 61.4 us -> 57.9 us
    pallas_call x1, Pallas kernels: 61.4 us -> 57.9 us  [on_device(): pl.pallas_call(kernel, out_shape=(jax.ShapeDtypeStruct(site_tensor.shape,...]
where the time goes in v2:
time: 62.3 us; the launch traced here: 62.1 us
  Pallas kernels  57.9 us (93%)
  local copies, waits for them, and re-layouts  3.54 us (6%)
  between operations  0.64 us (1%)
    pallas_call x1, Pallas kernels, on_device(): pl.pallas_call(kernel, out_shape=(jax.ShapeDtypeStruct(site_tensor.shape,...  57.9 us
    unnamed x2, local copies, waits for them, and re-layouts  3.54 us

profile of v2, /device:TPU:0, one launch (start us, length us, event | category | flops | bytes accessed | tf_op | source)
XLA Modules:
  0.0 62.1 jit_solution(11612695139698541775)
XLA Ops:
  0.6 57.9 %bond_update.1 = (f32[1,2,256,256]{3,2,1,0:T(8,128)}, f32[1,256,256]{2,1,0:T(8,128)}) custom-call(s32[16]{0:T(128)} %size_ref.1, f32[1,2,256,256]{3,2,1,0:T(8,128)} %site_hbm.1, f32[1,14,256,256]{3,2,1,0:T(8,128)} %left_hbm.1, f32[1,14,256,256]{3,2,1,0:T(8,128)} %right_hbm.1), custom_call_target="tpu_custom_call" | custom-call | tf_op jit(solution)/shard_map/bond_update/pallas_call | solution.py:377
  58.5 1.9 %copy.8 = f32[1,2,256,256]{3,2,1,0:T(8,128)} copy(f32[1,2,256,256]{3,2,1,0:T(8,128)} %get-tuple-element.4) | data formatting | bytes 1048576
  60.4 1.7 %copy.9 = f32[1,256,256]{2,1,0:T(8,128)} copy(f32[1,256,256]{2,1,0:T(8,128)} %get-tuple-element.5) | data formatting | bytes 524288

commit v3 on v2

--- a/solution.py
+++ b/solution.py
@@ -84,8 +84,8 @@
 
 def kernel(
     size_ref, site_hbm, left_hbm, right_hbm,
-    out_hbm, bond_out,
-    site, low, left_f, right_f, left_s, right_s, aug, fac, packed, bond, applied, acc, field_in, field_s, low_out, up_out,
+    left_out, bond_out,
+    site, low, left_f, right_f, left_s, right_s, aug, fac, packed, bond, applied, acc, field_in, field_s,
     red_in, red_own, local_sem, send_sem, recv_sem, red_send, red_recv,
 ):
     count = lax.axis_size("row")
@@ -211,9 +211,7 @@
     bond[...] = jnp.where(live_pair & (column >= row), fac[:, :states], 0.0)
     inverse = jnp.where(column <= row, fac[:, states:], 0.0)
     turned = (((1,), (1,)), ((), ()))
-    up_out[...] = lax.dot_general(site[0], inverse, turned, precision=highest, preferred_element_type=f32)
-    store_up = pltpu.make_async_copy(up_out, out_hbm.at[0, 0], local_sem.at[3])
-    store_up.start()
+    left_out[0] = lax.dot_general(site[0], inverse, turned, precision=highest, preferred_element_type=f32)
 
     def put_field(which, value):
         field_s[which, 0], field_s[which, 1] = split_2(value)
@@ -275,9 +273,7 @@
     near_inverse = jnp.where(column < row, near, jnp.where(column == row, 1.0 / near, 0.0))
     outer = jnp.where((row < size) & (column < size_after), site[1], 0.0)
     outer = lax.dot_general(outer, near_inverse, turned, precision=highest, preferred_element_type=f32)
-    low_out[...] = jnp.where(not_last, outer, 0.0)
-    store_low = pltpu.make_async_copy(low_out, out_hbm.at[0, 1], local_sem.at[4])
-    store_low.start()
+    left_out[1] = jnp.where(not_last, outer, 0.0)
     for k in range(max(W_DN - early_down, W_UP - early_up)):
         down = [early_down + k] if early_down + k < W_DN else []
         up = [W_DN + early_up + k] if early_up + k < W_UP else []
@@ -360,12 +356,21 @@
         for one in leftward:
             one.wait_send()
 
-    store_low.wait()
-    store_up.wait()
     final_norm = full_sum(collect(1, second_sums)[:8])
-    bond_out[0] = acc[...] * jnp.sqrt(start_norm / final_norm)
+    bond_out[...] = acc[...] * jnp.sqrt(start_norm / final_norm)
     for one in first_sums + second_sums:
         one.wait_send()
+
+
+def write_out(left, bond, left_hbm, bond_hbm, sem):
+    stores = [
+        pltpu.make_async_copy(left, left_hbm.at[0], sem.at[0]),
+        pltpu.make_async_copy(bond, bond_hbm.at[0], sem.at[1]),
+    ]
+    for store in stores:
+        store.start()
+    for store in stores:
+        store.wait()
 
 
 def on_device(site_tensor, left_env, right_env, sector_size):
@@ -374,14 +379,15 @@
     count = lax.axis_size("row")
     block = (states, states)
     anywhere = pl.BlockSpec(memory_space=pl.ANY)
-    return pl.pallas_call(
+    inside = pl.BlockSpec(memory_space=pltpu.VMEM)
+    left_out, bond_out = pl.pallas_call(
         kernel,
         out_shape=(
-            jax.ShapeDtypeStruct(site_tensor.shape, f32),
-            jax.ShapeDtypeStruct((1,) + block, f32),
+            pltpu.VMEM((2,) + block, f32),
+            pltpu.VMEM(block, f32),
         ),
-        in_specs=[pl.BlockSpec(memory_space=pltpu.SMEM), anywhere, anywhere, anywhere],
-        out_specs=(anywhere, pl.BlockSpec(memory_space=pltpu.VMEM)),
+        in_specs=[pl.BlockSpec(memory_space=pltpu.SMEM)] + [pl.BlockSpec(memory_space=pltpu.HBM)] * 3,
+        out_specs=(inside, inside),
         scratch_shapes=[
             pltpu.VMEM((2,) + block, f32),
             pltpu.VMEM(block, f32),
@@ -397,21 +403,31 @@
             pltpu.VMEM(block, f32),
             pltpu.VMEM((2, 2) + block, f32),
             pltpu.VMEM((3, 2) + block, bf16),
-            pltpu.VMEM(block, f32),
-            pltpu.VMEM(block, f32),
             pltpu.VMEM((2, count, 16, 128), f32),
             pltpu.VMEM((2, 16, 128), f32),
-            pltpu.SemaphoreType.DMA((5,)),
+            pltpu.SemaphoreType.DMA((3,)),
             pltpu.SemaphoreType.DMA((W_DN + W_UP + 6,)),
             pltpu.SemaphoreType.DMA((W_DN + W_UP + 6,)),
             pltpu.SemaphoreType.DMA((2, count)),
             pltpu.SemaphoreType.DMA((2, count)),
         ],
         compiler_params=pltpu.CompilerParams(
-            collective_id=0, has_side_effects=True, vmem_limit_bytes=56 * 1024 * 1024
+            collective_id=0, has_side_effects=True, vmem_limit_bytes=60 * 1024 * 1024
         ),
         name="bond_update",
     )(sector_size, site_tensor, left_env, right_env)
+    return pl.pallas_call(
+        write_out,
+        out_shape=(
+            jax.ShapeDtypeStruct(site_tensor.shape, f32),
+            jax.ShapeDtypeStruct((1,) + block, f32),
+        ),
+        in_specs=[inside, inside],
+        out_specs=(anywhere, anywhere),
+        scratch_shapes=[pltpu.SemaphoreType.DMA((2,))],
+        compiler_params=pltpu.CompilerParams(vmem_limit_bytes=4 * 1024 * 1024),
+        name="write_out",
+    )(left_out, bond_out)
 
 
 def solution(mesh):

time: 62.3 us -> 58.9 us (0.945)
  local copies, waits for them, and re-layouts: 3.54 us -> 0 us
    unnamed x2 -> x0, local copies, waits for them, and re-layouts: 3.54 us -> none
    pallas_call x1 -> x2, Pallas kernels: 57.9 us -> 58.1 us  [the longest x1 57.2 us: on_device(): pl.pallas_call(kernel, out_shape=(pltpu.VMEM((2,) + block, f32), pltpu.VM...]
where the time goes in v3:
time: 58.9 us; the launch traced here: 58.7 us
  Pallas kernels  58.1 us (99%)
  between operations  0.64 us (1%)
    pallas_call x1, Pallas kernels, on_device(): pl.pallas_call(kernel, out_shape=(pltpu.VMEM((2,) + block, f32), pltpu.VM...  57.2 us

profile of v3, /device:TPU:0, one launch (start us, length us, event | category | flops | bytes accessed | tf_op | source)
XLA Modules:
  0.0 58.7 jit_solution(12437085581497293654)
XLA Ops:
  0.6 57.2 %bond_update.1 = (f32[2,256,256]{2,1,0:T(8,128)S(1)}, f32[256,256]{1,0:T(8,128)S(1)}) custom-call(s32[16]{0:T(128)} %size_ref.1, f32[1,2,256,256]{3,2,1,0:T(8,128)} %site_hbm.1, f32[1,14,256,256]{3,2,1,0:T(8,128)} %left_hbm.1, f32[1,14,256,256]{3,2,1,0:T(8,128)} %right_hbm.1), custom_call_target="tpu_custom_call" | custom-call | tf_op jit(solution)/shard_map/bond_update/pallas_call | solution.py:383
  57.8 0.9 %write_out.1 = (f32[1,2,256,256]{3,2,1,0:T(8,128)}, f32[1,256,256]{2,1,0:T(8,128)}) custom-call(f32[2,256,256]{2,1,0:T(8,128)S(1)} %get-tuple-element.4.left, f32[256,256]{1,0:T(8,128)S(1)} %get-tuple-element.5.bond), custom_call_target="tpu_custom_call" | custom-call | tf_op jit(solution)/shard_map/write_out/pallas_call | solution.py:419
